TPU v7x, 128 devices: a whole 4x4x4 slice. The times are simulated.
128 devices in a mesh: tp: 16 (over z, y), dp: 8 (over x, core).
Axes of the slice: x: 4, y: 4, z: 4, core: 2. Of those that a mesh axis runs over, the one named last changes fastest.
Arguments:
- hidden: bfloat16 [8192, 576], P('dp')
- norm_w: bfloat16 [576], replicated
- emb_table: bfloat16 [49152, 576], P('tp')
- teacher: bfloat16 [8192, 49152], P('dp', 'tp')
- loss_mask: int32 [8192], P('dp')
Outputs:
- output 1: float32 [], replicated
- output 2: bfloat16 [8192, 576], P('dp')
- output 3: float32 [49152, 576], P('tp', 'dp')
- output 4: float32 [576], replicated
All inputs are finite; a program needn't handle non-finite values.
Results may differ from a plain program's by a relative error of at most 0.001.
Values sent between devices are 32-bit elements.
A program may use at most 1 GiB of HBM per device.

v0:
```python
import jax
import jax.numpy as jnp
from jax import lax
from jax.sharding import PartitionSpec as P

SOFT_CAP = 30.0
NORM_EPS = 1e-6


def rms_norm(hid_f32, scale_f32):
    inv_rms = lax.rsqrt(jnp.mean(hid_f32 * hid_f32, axis=-1, keepdims=True) + NORM_EPS)
    return hid_f32 * inv_rms * (1.0 + scale_f32)


def solution(mesh):
    def device_fn(hid_loc, norm_w, emb_loc, teach_loc, mask_loc):
        mask_f32 = mask_loc.astype(jnp.float32)
        tok_count = lax.psum(jnp.sum(mask_f32), 'dp')
        weight = mask_f32 / tok_count
        normed_f32, norm_pull = jax.vjp(rms_norm, hid_loc.astype(jnp.float32), norm_w.astype(jnp.float32))
        normed = normed_f32.astype(jnp.bfloat16)
        raw_logit = jnp.einsum('nd,vd->nv', normed, emb_loc, preferred_element_type=jnp.float32)
        tanh_val = jnp.tanh(raw_logit / SOFT_CAP)
        capped = SOFT_CAP * tanh_val
        teach_f32 = teach_loc.astype(jnp.float32)
        maxima = lax.pmax(jnp.stack([jnp.max(capped, axis=-1), jnp.max(teach_f32, axis=-1)], axis=-1), 'tp')
        stu_exp = jnp.exp(capped - maxima[:, 0:1])
        tea_exp = jnp.exp(teach_f32 - maxima[:, 1:2])
        local_sums = jnp.stack([jnp.sum(stu_exp, axis=-1), jnp.sum(tea_exp, axis=-1), jnp.sum(tea_exp * (teach_f32 - capped), axis=-1)], axis=-1)
        totals = lax.psum(local_sums, 'tp')
        lse_stu = maxima[:, 0] + jnp.log(totals[:, 0])
        lse_tea = maxima[:, 1] + jnp.log(totals[:, 1])
        kl_tok = totals[:, 2] / totals[:, 1] - lse_tea + lse_stu
        loss_val = lax.psum(jnp.sum(weight * kl_tok), 'dp')
        prob_diff = stu_exp / totals[:, 0:1] - tea_exp / totals[:, 1:2]
        d_raw = (prob_diff * weight[:, None] * (1.0 - tanh_val * tanh_val)).astype(jnp.bfloat16)
        grad_normed = lax.psum(jnp.dot(d_raw, emb_loc, preferred_element_type=jnp.float32), 'tp')
        emb_part = jnp.einsum('nv,nd->vd', d_raw, normed, preferred_element_type=jnp.float32)
        grad_emb = lax.psum_scatter(emb_part, 'dp', scatter_dimension=1, tiled=True)
        grad_hid, grad_scale = norm_pull(grad_normed)
        grad_w = lax.psum(grad_scale, 'dp')
        return loss_val, grad_hid.astype(jnp.bfloat16), grad_emb, grad_w

    return jax.shard_map(device_fn, mesh=mesh, in_specs=(P('dp', None), P(None), P('tp', None), P('dp', 'tp'), P('dp')), out_specs=(P(), P('dp', None), P('tp', 'dp'), P(None)), check_vma=False)
```

profile of v0, /device:TPU:1, one launch (start us, length us, event | category | flops | bytes accessed | tf_op | source)
XLA Modules:
  0.0 302.1 jit_solution(6202979873798799374)
XLA Ops:
  8.0 0.0 copy-start
  8.0 0.0 copy-start.4
  8.0 0.0 all-reduce.3.cloned.1.call-start
  8.1 1.4 convert_reduce_fusion
  9.5 13.8 %psum.35 = f32[]{:T(128)} all-reduce(f32[]{:T(128)} %convert_reduce_fusion), channel_id=1, replica_groups=mesh['tp'=16,'dp'=8] {'dp'}, use_global_device_ids=true, to_apply=%region_1.0 | all-reduce | flops 1 | bytes 8 | tf_op jit(solution)/shard_map/psum | solution.py:18
  23.3 3.7 %reduce_max.26 = bf16[1024]{0:T(1024)(128)(2,1)S(1)} reduce(bf16[1024,3072]{1,0:T(8,128)(2,1)} %param.8, bf16[]{:T(256)} %constant.19.clone.1), dimensions={1}, to_apply=%region_4.0 | reduce | flops 3144704 | bytes 6293506 | tf_op jit(solution)/shard_map/reduce_max | solution.py:26
  27.0 0.0 copy-done.4
  27.0 1.5 fusion.17
  28.6 0.0 copy-done
  28.6 0.0 copy-start.2
  28.6 10.2 %fusion.11 = (f32[1024]{0:T(1024)S(1)}, f32[1024,3072]{1,0:T(8,128)}) fusion(bf16[3072,576]{0,1:T(8,128)(2,1)S(1)} %copy-done, bf16[1024,576]{0,1:T(8,128)(2,1)} %param.5, f32[576]{0:T(1024)S(1)} %convert_add_fusion, f32[1024]{0:T(1024)S(1)} %fusion.23), kind=kOutput, calls=%fused_computation.15 | convolution fusion | flops 3635674112 | bytes 17312000 | tf_op jit(solution)/shard_map/nd,vd->nv/dot_general | solution.py:22
  38.8 0.0 copy-done.2
  38.8 36.1 %pmax.7 = f32[1024,2]{0,1:T(2,128)} all-reduce(f32[1024,2]{0,1:T(2,128)S(1)} %pad_maximum_fusion.1), channel_id=1, replica_groups=mesh['tp'=16,'dp'=8] {'tp'}, use_global_device_ids=true, to_apply=%region_5.0 | all-reduce | flops 2048 | bytes 16384 | tf_op jit(solution)/shard_map/pmax | solution.py:26
  74.9 0.8 fusion.25
  75.7 11.6 %fusion.10 = (f32[1024]{0:T(1024)S(1)}, f32[1024]{0:T(1024)S(1)}, f32[1024]{0:T(1024)S(1)}) fusion(f32[1024,3072]{1,0:T(8,128)} %get-tuple-element.19, f32[1024]{0:T(1024)S(1)} %bitcast.17, f32[1024]{0:T(1024)S(1)} %bitcast.14, bf16[1024,3072]{1,0:T(8,128)(2,1)} %param.8), kind=kLoop, calls=%fused_computation.14 | loop fusion | flops 31454208 | bytes 18894848 | tf_op jit(solution)/shard_map/reduce_sum | solution.py:29
  87.3 0.6 pad_maximum_fusion
  87.9 56.1 %psum.36 = f32[1024,3]{0,1:T(4,128)} all-reduce(f32[1024,3]{0,1:T(4,128)} %pad_maximum_fusion), channel_id=1, replica_groups=mesh['tp'=16,'dp'=8] {'tp'}, use_global_device_ids=true, to_apply=%region_9.0 | all-reduce | flops 3072 | bytes 24576 | tf_op jit(solution)/shard_map/psum | solution.py:30
  144.0 0.8 fusion.24
  144.8 1.9 multiply_reduce_fusion
  146.7 11.3 %fusion.8 = bf16[1024,3072]{1,0:T(8,128)(2,1)S(1)} fusion(bf16[1024,3072]{1,0:T(8,128)(2,1)} %param.8, f32[1024,3072]{1,0:T(8,128)} %get-tuple-element.19, f32[1024]{0:T(1024)S(1)} %get-tuple-element.12, f32[1024]{0:T(1024)S(1)} %bitcast.23, f32[1024]{0:T(1024)S(1)} %bitcast.21, f32[1024]{0:T(1024)S(1)} %bitcast.16, f32[1024]{0:T(1024)S(1)} %bitcast.19), kind=kLoop, calls=%fused_computation.12 | loop fusion | flops 40894464 | bytes 25186304 | tf_op jit(solution)/shard_map/convert_element_type | solution.py:36
  158.1 0.0 copy-start.1
  158.1 2.7 copy-done.1
  160.8 0.0 copy-start.3
  160.8 5.2 %fusion.26 = f32[1024,576]{0,1:T(8,128)} fusion(bf16[1024,3072]{1,0:T(8,128)(2,1)S(1)} %fusion.8, bf16[3072,576]{0,1:T(8,128)(2,1)S(1)} %copy-done), kind=kOutput, calls=%fused_computation.41 | convolution fusion | flops 3623878656 | bytes 12189696 | tf_op jit(solution)/shard_map/dot_general | solution.py:37
  166.0 0.0 all-reduce.3.cloned.1.call-update
  166.0 0.0 reduce-scatter.2.cloned.1.call-start
  166.1 0.0 copy-done.3
  166.1 10.0 %fusion.19 = f32[3072,576]{0,1:T(8,128)} fusion(bf16[1024,3072]{1,0:T(8,128)(2,1)} %copy-done.1, bf16[1024,576]{0,1:T(8,128)(2,1)} %param.5, f32[576]{0:T(1024)S(1)} %convert_add_fusion, f32[1024]{0:T(1024)S(1)} %copy-done.3), kind=kOutput, calls=%fused_computation.28 | convolution fusion | flops 3626237952 | bytes 14555392 | tf_op jit(solution)/shard_map/nv,nd->vd/dot_general | solution.py:38
  176.0 0.0 reduce-scatter.2.cloned.1.call-update
  176.1 96.9 %all-reduce.3.cloned.1.call-done = f32[1024,576]{0,1:T(8,128)} async-done(((f32[1024,576]{0,1:T(8,128)}), f32[1024,576]{0,1:T(8,128)}) %all-reduce.3.cloned.1.call-update) | async-done | bytes 2359312 | tf_op jit(solution)/shard_map/psum | solution.py:37
  273.0 3.4 %fusion.15 = (f32[576]{0:T(1024)}, f32[1024]{0:T(1024)S(1)}) fusion(f32[1024,576]{0,1:T(8,128)} %all-reduce.3.cloned.1.call-done, bf16[1024,576]{0,1:T(8,128)(2,1)} %param.5, f32[1024]{0:T(1024)S(1)} %copy-done.3, f32[576]{0:T(1024)S(1)} %convert_add_fusion), kind=kLoop, calls=%fused_computation.24 | loop fusion | flops 4127168 | bytes 3551744 | tf_op jit(solution)/shard_map/transpose(jvp())/reduce_sum | solution.py:12
  276.3 14.7 %all-reduce = (f32[]{:T(128)}, f32[576]{0:T(1024)}) all-reduce(f32[]{:T(128)} %get-tuple-element.11, f32[576]{0:T(1024)} %get-tuple-element.7), channel_id=1, replica_groups=mesh['tp'=16,'dp'=8] {'dp'}, use_global_device_ids=true, to_apply=%region_11.0 | all-reduce | flops 577 | bytes 4616 | tf_op jit(solution)/shard_map/psum | solution.py:34
  291.0 3.6 %fusion.16 = bf16[1024,576]{0,1:T(8,128)(2,1)} fusion(bf16[1024,576]{0,1:T(8,128)(2,1)} %param.5, f32[1024,576]{0,1:T(8,128)} %all-reduce.3.cloned.1.call-done, f32[1024]{0:T(1024)S(1)} %multiply_multiply_fusion, f32[576]{0:T(1024)S(1)} %convert_add_fusion, f32[1024]{0:T(1024)S(1)} %copy-done.3), kind=kLoop, calls=%fused_computation.25 | loop fusion | flops 4128768 | bytes 4729088 | tf_op jit(solution)/shard_map/convert_element_type | solution.py:42
  294.6 0.0 reduce-scatter.2.cloned.1.call-done
  (5 shorter events, 0.0 us)
Async XLA Ops:
  8.0 20.6 %copy-start = (bf16[3072,576]{0,1:T(8,128)(2,1)S(1)}, bf16[3072,576]{0,1:T(8,128)(2,1)}, u32[]{:S(2)}) copy-start(bf16[3072,576]{0,1:T(8,128)(2,1)} %param.7) | copy-start | bytes 10616836
  8.0 19.0 %copy-start.4 = (bf16[576]{0:T(1024)(128)(2,1)S(1)}, bf16[576]{0:T(1024)(128)(2,1)}, u32[]{:S(2)}) copy-start(bf16[576]{0:T(1024)(128)(2,1)} %param.6) | copy-start | bytes 3460
  8.0 264.9 %all-reduce.3.cloned.1.call-start = ((), (), s32[]{:S(2)}) async-start(), calls=%async_computation.1 | async-start | bytes 4718592 | tf_op jit(solution)/shard_map/psum | solution.py:37
  28.6 10.2 %copy-start.2 = (f32[1024]{0:T(1024)}, f32[1024]{0:T(1024)S(1)}, u32[]{:S(2)}) copy-start(f32[1024]{0:T(1024)S(1)} %fusion.23) | copy-start | bytes 12292
  158.1 2.7 copy-start.1
  160.8 5.3 %copy-start.3 = (f32[1024]{0:T(1024)S(1)}, f32[1024]{0:T(1024)}, u32[]{:S(2)}) copy-start(f32[1024]{0:T(1024)} %copy-done.2) | copy-start | bytes 12292
  166.0 128.6 %reduce-scatter.2.cloned.1.call-start = ((), (), s32[]{:S(2)}) async-start(), calls=%async_computation.2 | async-start | bytes 7962624 | tf_op jit(solution)/shard_map/reduce_scatter | solution.py:39
Sparse Core Ops, SparseCore 0:
  166.1 106.7 all-reduce.2
Sparse Core Ops, SparseCore 1:
  176.2 61.9 reduce-scatter.1
where the time goes:
time: 303 us; the launch traced here: 302 us
  blocking collectives  121 us (40%)
  waiting for transfers between devices  96.9 us (32%)
  other arithmetic  39.2 us (13%)
  matrix products  25.4 us (8%)
  between operations  15.6 us (5%)
  local copies, waits for them, and re-layouts  4.3 us (1%)
    psum x1, waiting for transfers between devices, device_fn(): lax.psum(jnp.dot(d_raw, emb_loc, preferred_element_type=jnp.float32), 'tp')  96.9 us
    psum x1, blocking collectives, device_fn(): totals = lax.psum(local_sums, 'tp')  56.1 us
    pmax x1, blocking collectives, device_fn(): lax.pmax(jnp.stack([jnp.max(capped, axis=-1), jnp.max(teach_f32, axis=-1)...  36.1 us
    psum x1, blocking collectives, device_fn(): loss_val = lax.psum(jnp.sum(weight * kl_tok), 'dp')  14.7 us
    psum x1, blocking collectives, device_fn(): tok_count = lax.psum(jnp.sum(mask_f32), 'dp')  13.8 us
    reduce_sum x1, other arithmetic, device_fn(): jnp.sum(stu_exp, axis=-1)  11.6 us
    convert_element_type x1, other arithmetic, device_fn(): (prob_diff * weight[:, None] * (1.0 - tanh_val * tanh_val)).astype(jnp.bf...  11.3 us
    dot_general x1, matrix products, device_fn(): jnp.einsum('nd,vd->nv', normed, emb_loc, preferred_element_type=jnp.float32)  10.2 us
  transfers between devices with their start and end apart: 2, of which 1 were waited for; matrix products, arithmetic and copies ran while one was open for 6% of the time, Pallas kernels for 0%

commit v1 on v0

v1 whole, which is shorter than its diff:
```python
import jax
import jax.numpy as jnp
from jax import lax
from jax.experimental import pallas as pl
from jax.experimental.pallas import tpu as pltpu
from jax.sharding import PartitionSpec as P

CAP = 30.0
EPS = 1e-6
LOG2E = 1.4426950408889634
MESH = pl.DeviceIdType.MESH
F32 = jnp.float32
BF16 = jnp.bfloat16
RB = 32


def build(tok, dim, voc, nt, nd):
    side = 4
    ht = tok // 2
    zc = ht // side
    oc = zc // side
    zh = zc // 2
    cols = dim // nd
    nv = 4
    vc = voc // nv
    vh = vc // 2
    vb = 512 if voc % 512 == 0 else 128
    nvb = voc // vb
    half_d = dim // 2
    dpad = -(-dim // 128) * 128

    def kernel(hid, w_ref, mask_ref, e_hbm, t_hbm, loss_out, dh_out, det_out, dw_out,
               e_v, t_v, gb, gt, tv, dr, dg, dhf, acc, mcol, col, st_s, st_r, mk_s, mk_r, dwt_s, dwt_r, dwd_s, dwd_r,
               zr, p2r, det, d2r, xr,
               in_sem, ss_st, rs_st, ss_mk, rs_mk, ss_z, rs_z, ss_p, rs_p, ss_g, rs_g, ss_h, rs_h,
               ss_d, rs_d, ss_x, rs_x, ss_wt, rs_wt, ss_wd, rs_wd):
        t = lax.axis_index('tp')
        d = lax.axis_index('dp')
        z, y = t // side, lax.rem(t, side)
        x, c = d // 2, lax.rem(d, 2)
        sends = []

        def rcopy(src, dst, ssem, rsem, dev):
            cp = pltpu.make_async_remote_copy(src_ref=src, dst_ref=dst, send_sem=ssem, recv_sem=rsem,
                                              device_id=dev, device_id_type=MESH)
            cp.start()
            sends.append(cp)
            return cp

        in_cp = [pltpu.make_async_copy(e_hbm, e_v, in_sem.at[0])]
        for h in range(2):
            rows = pl.ds(h * ht, ht)
            in_cp.append(pltpu.make_async_copy(t_hbm.at[rows, :], t_v.at[rows, :], in_sem.at[1 + h]))
        for cp in (in_cp[1], in_cp[0], in_cp[2]):
            cp.start()

        barrier = pltpu.get_barrier_semaphore()
        for k in range(1, nt):
            pl.semaphore_signal(barrier, inc=1, device_id={'tp': lax.rem(t + k, nt), 'dp': d}, device_id_type=MESH)
        for k in range(1, nd):
            pl.semaphore_signal(barrier, inc=1, device_id={'tp': t, 'dp': lax.rem(d + k, nd)}, device_id_type=MESH)

        wp = 1.0 + w_ref[...].astype(F32)
        nb = min(256, tok)

        for i in range(tok // nb):
            r0 = i * nb
            xv = hid[r0:r0 + nb, :].astype(F32)
            s = lax.rsqrt(jnp.mean(xv * xv, axis=-1, keepdims=True) + EPS)
            g = xv * s * wp
            gb[r0:r0 + nb, :] = g.astype(BF16)
            gp = jnp.concatenate([g, jnp.zeros((nb, dpad - dim), F32)], axis=1) if dpad > dim else g
            gtv = gp.T
            gtv = jnp.concatenate([gtv[(2 * xx + cc) * cols:(2 * xx + cc + 1) * cols, :] for cc in range(2) for xx in range(side)], axis=0)
            gt[:, r0:r0 + nb] = gtv.astype(BF16)

        maskf = mask_ref[...].astype(F32)
        mk_s[...] = jnp.broadcast_to(jnp.sum(maskf, axis=1, keepdims=True), (8, 128))
        mk_r[d] = mk_s[...]
        pl.semaphore_wait(barrier, nt + nd - 2)
        mk_cp = [rcopy(mk_s, mk_r.at[d], ss_mk.at[k], rs_mk.at[k], {'tp': t, 'dp': lax.rem(d + k, nd)}) for k in range(1, nd)]

        def forward(h):
            base = h * ht
            in_cp[1 + h].wait()
            if h == 0:
                in_cp[0].wait()

            def mx(i, _):
                r = pl.multiple_of(base + i * 64, 64)
                m = t_v[pl.ds(r, 64), 0:128]
                for q in range(1, voc // 128):
                    m = jnp.maximum(m, t_v[pl.ds(r, 64), q * 128:(q + 1) * 128])
                mm = jnp.max(m.astype(F32), axis=1, keepdims=True)
                mcol[pl.ds(pl.multiple_of(i * 64, 64), 64), :] = jnp.broadcast_to(mm, (64, 128))
                return 0

            lax.fori_loop(0, ht // 64, mx, 0)
            acc[...] = jnp.zeros_like(acc)

            def vstep(b, _):
                v0 = pl.multiple_of(b * vb, vb)
                tv[pl.ds(base, ht), pl.ds(v0, vb)] = lax.dot_general(
                    gb[pl.ds(base, ht), :], e_v[pl.ds(v0, vb), :], (((1,), (1,)), ((), ())), preferred_element_type=F32)

                def rstep(i, _):
                    r = pl.multiple_of(base + i * RB, RB)
                    a = pl.ds(pl.multiple_of(i * RB, RB), RB)
                    m = mcol[a, :]
                    zs = jnp.zeros((RB, 128), F32)
                    zt = jnp.zeros((RB, 128), F32)
                    qs = jnp.zeros((RB, 128), F32)
                    for q in range(vb // 128):
                        lanes = pl.ds(pl.multiple_of(v0 + q * 128, 128), 128)
                        th = jnp.tanh(tv[pl.ds(r, RB), lanes] * (1.0 / CAP))
                        tv[pl.ds(r, RB), lanes] = th
                        u = t_v[pl.ds(r, RB), lanes].astype(F32) - m
                        et = jnp.exp2(u * LOG2E)
                        zs = zs + jnp.exp2(th * (CAP * LOG2E))
                        zt = zt + et
                        qs = qs + et * (u - CAP * th)
                    acc[0, a, :] += zs
                    acc[1, a, :] += zt
                    acc[2, a, :] += qs
                    return 0

                lax.fori_loop(0, ht // RB, rstep, 0)
                return 0

            lax.fori_loop(0, nvb, vstep, 0)
            parts = [mcol[...].T[0:1, :]] + [jnp.sum(acc[k].T, axis=0, keepdims=True) for k in range(3)]
            st_s[h] = jnp.concatenate(parts + [jnp.zeros((4, ht), F32)], axis=0)
            st_r[h, t] = st_s[h]
            return [rcopy(st_s.at[h], st_r.at[h, t], ss_st.at[h, k], rs_st.at[h, k], {'tp': lax.rem(t + k, nt), 'dp': d})
                    for k in range(1, nt)]

        def combine(h, cps, inv_m):
            for cp in cps:
                cp.wait_recv()
            mts = st_r[h, :, 0, :]
            mt = jnp.max(mts, axis=0, keepdims=True)
            dm = jnp.maximum(mts - mt, -3e38)
            e = jnp.exp(dm)
            zte = st_r[h, :, 2, :] * e
            zt = jnp.sum(zte, axis=0, keepdims=True)
            zs = jnp.sum(st_r[h, :, 1, :], axis=0, keepdims=True)
            a = jnp.sum(st_r[h, :, 3, :] * e + zte * dm, axis=0, keepdims=True)
            kl = a / zt - jnp.log(zt) + jnp.log(zs)
            w = maskf[:, h * ht:(h + 1) * ht] * inv_m
            for k, row in enumerate((w / zs, w / zt, mt)):
                col[k, h * ht:(h + 1) * ht, :] = jnp.broadcast_to(row, (128, ht)).T
            return jnp.sum(w * kl, axis=1, keepdims=True)

        def backward(h):
            base = h * ht

            def vstep(b, _):
                v0 = pl.multiple_of(b * vb, vb)

                def rstep(i, _):
                    r = pl.ds(pl.multiple_of(base + i * RB, RB), RB)
                    cs, ct, m = col[0, r, :], col[1, r, :], col[2, r, :]
                    for q in range(vb // 128):
                        lanes = pl.ds(pl.multiple_of(v0 + q * 128, 128), 128)
                        th = tv[r, lanes]
                        ps = jnp.exp2(th * (CAP * LOG2E)) * cs
                        pt = jnp.exp2((t_v[r, lanes].astype(F32) - m) * LOG2E) * ct
                        dr[r, lanes] = ((ps - pt) * (1.0 - th * th)).astype(BF16)
                    return 0

                lax.fori_loop(0, ht // RB, rstep, 0)
                return 0

            lax.fori_loop(0, nvb, vstep, 0)
            dg[pl.ds(base, ht), :] = jnp.dot(dr[pl.ds(base, ht), :], e_v[...], preferred_element_type=F32)

        p1 = (z, y)
        p2 = (y, z)

        def tp1(h, q):
            return {'tp': q * side + y if h == 0 else z * side + q, 'dp': d}

        def tp2(h, q):
            return {'tp': z * side + q if h == 0 else q * side + y, 'dp': d}

        def hrows(h, q, o, n):
            return pl.ds(pl.multiple_of(h * ht + q * zc + o, 8), n)

        def rs_start(h):
            p = p1[h]
            nxt, prv, opp = lax.rem(p + 1, side), lax.rem(p + 3, side), lax.rem(p + 2, side)
            cps = {}
            for name, dirn, q, o, dev in (('a', 0, opp, 0, nxt), ('a', 1, opp, zh, prv), ('b', 0, nxt, zh, nxt), ('b', 1, prv, 0, prv)):
                slot = 'abc'.index(name) * 2 + dirn
                cps[name, dirn] = rcopy(dg.at[hrows(h, q, o, zh), :], zr.at[h, slot], ss_z.at[h, slot], rs_z.at[h, slot], tp1(h, dev))
            return cps

        def rs_mid(h, cps):
            p = p1[h]
            nxt, prv = lax.rem(p + 1, side), lax.rem(p + 3, side)
            for dirn, q, o, dev in ((0, nxt, 0, nxt), (1, prv, zh, prv)):
                cps['a', dirn].wait_recv()
                dg[hrows(h, q, o, zh), :] += zr[h, dirn]
            for dirn, q, o, dev in ((0, nxt, 0, nxt), (1, prv, zh, prv)):
                slot = 4 + dirn
                cps['c', dirn] = rcopy(dg.at[hrows(h, q, o, zh), :], zr.at[h, slot], ss_z.at[h, slot], rs_z.at[h, slot], tp1(h, dev))

        def rs_end(h, cps):
            p = p1[h]
            for name in 'bc':
                for dirn in range(2):
                    cps[name, dirn].wait_recv()
            dg[hrows(h, p, 0, zh), :] += zr[h, 4] + zr[h, 3]
            dg[hrows(h, p, zh, zh), :] += zr[h, 2] + zr[h, 5]
            out = []
            for k in range(1, side):
                q = lax.rem(p2[h] + k, side)
                out.append(rcopy(dg.at[hrows(h, p, q * oc, oc), :], p2r.at[h, k - 1], ss_p.at[h, k - 1], rs_p.at[h, k - 1], tp2(h, q)))
            return out

        def norm_back(h, cps):
            for cp in cps:
                cp.wait_recv()
            rows = hrows(h, p1[h], p2[h] * oc, oc)
            gv = dg[rows, :] + p2r[h, 0] + p2r[h, 1] + p2r[h, 2]
            xv = hid[rows, :].astype(F32)
            s = lax.rsqrt(jnp.mean(xv * xv, axis=-1, keepdims=True) + EPS)
            cv = gv * wp
            m = jnp.mean(cv * xv, axis=-1, keepdims=True)
            dhf[rows, :] = s * cv - xv * (s * s * s * m)
            out = []
            for k in range(1, side):
                out.append(rcopy(dhf.at[rows, :], dhf.at[rows, :], ss_g.at[h, k - 1], rs_g.at[h, k - 1], tp2(h, lax.rem(p2[h] + k, side))))
            return out, jnp.sum(gv * xv * s, axis=0, keepdims=True)

        def ag_start(h, cps1):
            for cp in cps1:
                cp.wait_recv()
            p = p1[h]
            nxt, prv = lax.rem(p + 1, side), lax.rem(p + 3, side)
            cps = {}
            for name, dirn, o, dev in (('a', 0, 0, nxt), ('a', 1, zh, prv), ('b', 0, zh, nxt), ('b', 1, 0, prv)):
                slot = 'abc'.index(name) * 2 + dirn
                rows = hrows(h, p, o, zh)
                cps[name, dirn] = rcopy(dhf.at[rows, :], dhf.at[rows, :], ss_h.at[h, slot], rs_h.at[h, slot], tp1(h, dev))
            return cps

        def ag_mid(h, cps):
            p = p1[h]
            nxt, prv = lax.rem(p + 1, side), lax.rem(p + 3, side)
            for dirn, q, o, dev in ((0, prv, 0, nxt), (1, nxt, zh, prv)):
                cps['a', dirn].wait_recv()
                slot = 4 + dirn
                rows = hrows(h, q, o, zh)
                cps['c', dirn] = rcopy(dhf.at[rows, :], dhf.at[rows, :], ss_h.at[h, slot], rs_h.at[h, slot], tp1(h, dev))

        def ag_end(h, cps):
            for name in 'bc':
                for dirn in range(2):
                    cps[name, dirn].wait_recv()
            rows = pl.ds(h * ht, ht)
            dh_out[rows, :] = dhf[rows, :].astype(BF16)

        xn, xp, xo = lax.rem(x + 1, side), lax.rem(x + 3, side), lax.rem(x + 2, side)

        def piece(q):
            return pl.ds(pl.multiple_of(c * half_d + q * cols, 8), cols)

        lo, hi = pl.ds(0, vh), pl.ds(vh, vh)

        def de_start(j):
            det[j] = jnp.dot(gt[...], dr[:, j * vc:(j + 1) * vc], preferred_element_type=F32)
            other = pl.ds(pl.multiple_of((1 - c) * half_d, 8), half_d)
            return rcopy(det.at[j, other, :], d2r.at[j], ss_d.at[j], rs_d.at[j], {'tp': t, 'dp': x * 2 + 1 - c})

        def xsend(j, slot, q, lanes, dev):
            return rcopy(det.at[j, piece(q), lanes], xr.at[j, slot], ss_x.at[j, slot], rs_x.at[j, slot], {'tp': t, 'dp': dev * 2 + c})

        def x_start(j, cp):
            cp.wait_recv()
            mine = pl.ds(pl.multiple_of(c * half_d, 8), half_d)
            det[j, mine, :] += d2r[j]
            return {('a', 0): xsend(j, 0, xo, lo, xn), ('a', 1): xsend(j, 1, xo, hi, xp),
                    ('b', 0): xsend(j, 2, xn, hi, xn), ('b', 1): xsend(j, 3, xp, lo, xp)}

        def x_mid(j, cps):
            cps['a', 0].wait_recv()
            det[j, piece(xn), lo] += xr[j, 0]
            cps['a', 1].wait_recv()
            det[j, piece(xp), hi] += xr[j, 1]
            cps['c', 0] = xsend(j, 4, xn, lo, xn)
            cps['c', 1] = xsend(j, 5, xp, hi, xp)

        def x_end(j, cps):
            for name in 'bc':
                for dirn in range(2):
                    cps[name, dirn].wait_recv()
            det_out[:, j * vc:j * vc + vh] = det[j, piece(x), lo] + xr[j, 4] + xr[j, 3]
            det_out[:, j * vc + vh:(j + 1) * vc] = det[j, piece(x), hi] + xr[j, 2] + xr[j, 5]

        st0 = forward(0)
        st1 = forward(1)
        for cp in mk_cp:
            cp.wait_recv()
        inv_m = 1.0 / jnp.sum(mk_r[:, 0, :], axis=0, keepdims=True)[:, 0:1]
        loss = combine(0, st0, inv_m)
        backward(0)
        rs0 = rs_start(0)
        loss = loss + combine(1, st1, inv_m)
        backward(1)
        rs1 = rs_start(1)
        rs_mid(0, rs0)
        dd = [None] * nv
        xs = [None] * nv
        dd[0] = de_start(0)
        dd[1] = de_start(1)
        xs[0] = x_start(0, dd[0])
        rs_mid(1, rs1)
        dd[2] = de_start(2)
        xs[1] = x_start(1, dd[1])
        dd[3] = de_start(3)
        xs[2] = x_start(2, dd[2])
        xs[3] = x_start(3, dd[3])
        ph0 = rs_end(0, rs0)
        x_mid(0, xs[0])
        ph1 = rs_end(1, rs1)
        ag0, dw0 = norm_back(0, ph0)
        x_mid(1, xs[1])
        ag1, dw1 = norm_back(1, ph1)
        dwv = dw0 + dw1
        zero = jnp.zeros((8, 128), F32)
        dwt_s[...] = zero
        for k in range(dpad // 128):
            n = min(128, dim - k * 128)
            dwt_s[k:k + 1, 0:n] = dwv[:, k * 128:k * 128 + n]
        dwt_r[t] = dwt_s[...]
        wt = [rcopy(dwt_s, dwt_r.at[t], ss_wt.at[k], rs_wt.at[k], {'tp': lax.rem(t + k, nt), 'dp': d}) for k in range(1, nt)]
        gh0 = ag_start(0, ag0)
        gh1 = ag_start(1, ag1)
        x_mid(2, xs[2])
        ag_mid(0, gh0)
        ag_mid(1, gh1)
        x_mid(3, xs[3])
        for cp in wt:
            cp.wait_recv()
        dws = jnp.sum(dwt_r[...], axis=0)
        rowi = lax.broadcasted_iota(jnp.int32, (8, 128), 0)
        dwd_s[...] = jnp.where(rowi == 7, jnp.broadcast_to(loss, (8, 128)), dws)
        dwd_r[d] = dwd_s[...]
        wd = [rcopy(dwd_s, dwd_r.at[d], ss_wd.at[k], rs_wd.at[k], {'tp': t, 'dp': lax.rem(d + k, nd)}) for k in range(1, nd)]
        ag_end(0, gh0)
        ag_end(1, gh1)
        for j in range(nv):
            x_end(j, xs[j])
        for cp in wd:
            cp.wait_recv()
        dwf = jnp.sum(dwd_r[...], axis=0)
        loss_out[...] = dwf[7:8, 0:1]
        for k in range(dpad // 128):
            n = min(128, dim - k * 128)
            dw_out[:, k * 128:k * 128 + n] = dwf[k:k + 1, 0:n]
        for cp in sends:
            cp.wait_send()

    sem = pltpu.SemaphoreType.DMA
    scratch = [
        pltpu.VMEM((voc, dim), BF16), pltpu.VMEM((tok, voc), BF16), pltpu.VMEM((tok, dim), BF16), pltpu.VMEM((dim, tok), BF16),
        pltpu.VMEM((tok, voc), F32), pltpu.VMEM((tok, voc), BF16), pltpu.VMEM((tok, dim), F32), pltpu.VMEM((tok, dim), F32),
        pltpu.VMEM((3, ht, 128), F32), pltpu.VMEM((ht, 128), F32), pltpu.VMEM((3, tok, 128), F32),
        pltpu.VMEM((2, 8, ht), F32), pltpu.VMEM((2, nt, 8, ht), F32), pltpu.VMEM((8, 128), F32), pltpu.VMEM((nd, 8, 128), F32),
        pltpu.VMEM((8, 128), F32), pltpu.VMEM((nt, 8, 128), F32), pltpu.VMEM((8, 128), F32), pltpu.VMEM((nd, 8, 128), F32),
        pltpu.VMEM((2, 6, zh, dim), F32), pltpu.VMEM((2, 3, oc, dim), F32),
        pltpu.VMEM((nv, dim, vc), F32), pltpu.VMEM((nv, half_d, vc), F32), pltpu.VMEM((nv, 6, cols, vh), F32),
        sem((3,)), sem((2, nt)), sem((2, nt)), sem((nd,)), sem((nd,)), sem((2, 6)), sem((2, 6)), sem((2, 3)), sem((2, 3)),
        sem((2, 3)), sem((2, 3)), sem((2, 6)), sem((2, 6)), sem((nv,)), sem((nv,)), sem((nv, 6)), sem((nv, 6)),
        sem((nt,)), sem((nt,)), sem((nd,)), sem((nd,)),
    ]
    vm = pl.BlockSpec(memory_space=pltpu.VMEM)
    anys = pl.BlockSpec(memory_space=pl.ANY)
    return pl.pallas_call(
        kernel,
        out_shape=(jax.ShapeDtypeStruct((1, 1), F32), jax.ShapeDtypeStruct((tok, dim), BF16),
                   jax.ShapeDtypeStruct((cols, voc), F32), jax.ShapeDtypeStruct((1, dim), F32)),
        in_specs=[vm, vm, vm, anys, anys],
        out_specs=(vm, vm, vm, vm),
        scratch_shapes=scratch,
        compiler_params=pltpu.CompilerParams(collective_id=0, has_side_effects=True, vmem_limit_bytes=67043328),
        name='head',
    )


def solution(mesh):
    nt, nd = mesh.shape['tp'], mesh.shape['dp']

    def device_fn(hid, norm_w, emb, teach, mask):
        tok, dim = hid.shape
        voc = emb.shape[0]
        call = build(tok, dim, voc, nt, nd)
        loss, dh, det, dw = call(hid, norm_w.reshape(1, dim), mask.reshape(1, tok), emb, teach)
        return loss.reshape(()), dh, det.T, dw.reshape(dim)

    return jax.shard_map(device_fn, mesh=mesh, in_specs=(P('dp', None), P(None), P('tp', None), P('dp', 'tp'), P('dp')),
                         out_specs=(P(), P('dp', None), P('tp', 'dp'), P(None)), check_vma=False)
```

time: 303 us -> 104 us (0.34)
  blocking collectives: 121 us -> 0 us
  waiting for transfers between devices: 96.9 us -> 0 us
  Pallas kernels: 0 us -> 87.1 us
  other arithmetic: 39.2 us -> 0.61 us
  matrix products: 25.4 us -> 0 us
  between operations: 15.6 us -> 2.48 us
  local copies, waits for them, and re-layouts: 4.3 us -> 13.1 us
    psum x1 -> x0, waiting for transfers between devices: 96.9 us -> none  [device_fn(): lax.psum(jnp.dot(d_raw, emb_loc, preferred_element_type=jnp.float32), 'tp')]
    pallas_call x0 -> x1, Pallas kernels: none -> 87.1 us  [device_fn(): call(hid, norm_w.reshape(1, dim), mask.reshape(1, tok), emb, teach)]
    psum x3 -> x0, blocking collectives: 84.6 us -> none  [the longest x1 56.1 us: device_fn(): totals = lax.psum(local_sums, 'tp')]
    pmax x1 -> x0, blocking collectives: 36.1 us -> none  [device_fn(): lax.pmax(jnp.stack([jnp.max(capped, axis=-1), jnp.max(teach_f32, axis=-1)...]
    dot_general x3 -> x0, matrix products: 25.4 us -> none  [the longest x1 10.2 us: device_fn(): jnp.einsum('nd,vd->nv', normed, emb_loc, preferred_element_type=jnp.float32)]
    reduce_sum x5 -> x0, other arithmetic: 19.9 us -> none  [the longest x1 11.6 us: device_fn(): jnp.sum(stu_exp, axis=-1)]
    convert_element_type x2 -> x0, other arithmetic: 14.9 us -> none  [the longest x1 11.3 us: device_fn(): (prob_diff * weight[:, None] * (1.0 - tanh_val * tanh_val)).astype(jnp.bf...]
    unnamed x10 -> x8, local copies, waits for them, and re-layouts: 2.68 us -> 11.9 us
  transfers between devices with their start and end apart: 2 -> 0, of which waited for: 1 -> 0; matrix products, arithmetic and copies ran while one was open for 6% -> 0% of each run, Pallas kernels for 0% -> 0%
where the time goes in v1:
time: 104 us; the launch traced here: 103 us
  Pallas kernels  87.1 us (84%)
  local copies, waits for them, and re-layouts  13.1 us (13%)
  between operations  2.48 us (2%)
    pallas_call x1, Pallas kernels, device_fn(): call(hid, norm_w.reshape(1, dim), mask.reshape(1, tok), emb, teach)  87.1 us
    unnamed x8, local copies, waits for them, and re-layouts  11.9 us

profile of v1, /device:TPU:1, one launch (start us, length us, event | category | flops | bytes accessed | tf_op | source)
XLA Modules:
  0.0 103.3 jit_solution(1970971444347334543)
XLA Ops:
  0.6 1.3 %reshape.20.w_ref = bf16[1,576]{1,0:T(2,128)(2,1)} reshape(bf16[576]{0:T(1024)(128)(2,1)} %param.6) | data formatting | bytes 2304 | tf_op jit(solution)/shard_map/reshape | solution.py:399
  1.9 2.4 %copy.9.hid = bf16[1024,576]{1,0:T(8,128)(2,1)} copy(bf16[1024,576]{0,1:T(8,128)(2,1)} %param.5) | data formatting | bytes 2359296 | tf_op args[0]
  4.3 6.1 %copy.10.e_hbm = bf16[3072,576]{1,0:T(8,128)(2,1)} copy(bf16[3072,576]{0,1:T(8,128)(2,1)} %param.7) | data formatting | bytes 7077888 | tf_op args[2]
  10.4 87.1 %head.1 = (f32[1,1]{1,0:T(1,128)}, bf16[1024,576]{1,0:T(8,128)(2,1)}, f32[72,3072]{1,0:T(8,128)}, f32[1,576]{1,0:T(1,128)}) custom-call(bf16[1024,576]{1,0:T(8,128)(2,1)} %copy.9.hid, bf16[1,576]{1,0:T(2,128)(2,1)} %reshape.20.w_ref, s32[1,1024]{1,0:T(1,128)} %bitcast.4, bf16[3072,576]{1,0:T(8,128)(2,1)} %copy.10.e_hbm, bf16[1024,3072]{1,0:T(8,128)(2,1)} %t_hbm.1), custom_call_target="tpu_custom_call" | custom-call | tf_op jit(solution)/shard_map/head/pallas_call | solution.py:399
  97.5 0.0 copy-start.1
  97.5 0.0 copy-start
  97.5 2.5 %copy.11 = bf16[1024,576]{0,1:T(8,128)(2,1)} copy(bf16[1024,576]{1,0:T(8,128)(2,1)} %get-tuple-element.13) | data formatting | bytes 2359296
  100.0 0.0 copy-done.1
  100.0 0.6 reduce
  101.3 0.0 copy-done
  101.3 0.9 copy.15
Async XLA Ops:
  97.5 2.5 %copy-start.1 = (f32[1,576]{1,0:T(1,128)S(1)}, f32[1,576]{1,0:T(1,128)}, u32[]{:S(2)}) copy-start(f32[1,576]{1,0:T(1,128)} %get-tuple-element.11) | copy-start | bytes 6916
  97.5 3.8 %copy-start = (f32[72,3072]{1,0:T(8,128)S(1)}, f32[72,3072]{1,0:T(8,128)}, u32[]{:S(2)}) copy-start(f32[72,3072]{1,0:T(8,128)} %get-tuple-element.10) | copy-start | bytes 2654212

commit v2 on v0

v2 whole, which is shorter than its diff:
```python
import jax
import jax.numpy as jnp
from jax import lax
from jax.experimental import pallas as pl
from jax.experimental.pallas import tpu as pltpu
from jax.sharding import PartitionSpec as P

CAP = 30.0
EPS = 1e-6
LOG2E = 1.4426950408889634
MESH = pl.DeviceIdType.MESH
F32 = jnp.float32
BF16 = jnp.bfloat16
SIDE = 4
NV = 4


def build(tok, dim, voc, nt, nd):
    ht = tok // 2
    zc = ht // SIDE
    fp = dim // SIDE
    cols = dim // nd
    vc = voc // NV
    vh = vc // 2
    vb = 256
    nvb = voc // vb
    half_d = dim // 2
    dpad = -(-dim // 128) * 128

    def kernel(hid, w_ref, mask_ref, e_hbm, t_hbm, loss_out, dh_out, det_out, dw_out,
               et, t_v, gb, gt, tv, tx, scr, wpc, dg, dhf, acc, mcol, col, st_s, st_r, mk_s, mk_r, dwt_s, dwt_r, dwd_s, dwd_r,
               zr, p2r, agb, d2r, xr,
               in_sem, ss_st, rs_st, ss_mk, rs_mk, ss_z, rs_z, ss_p, rs_p, ss_g, rs_g, ss_h, rs_h,
               ss_d, rs_d, ss_x, rs_x, ss_wt, rs_wt, ss_wd, rs_wd):
        t = lax.axis_index('tp')
        d = lax.axis_index('dp')
        z, y = t // SIDE, lax.rem(t, SIDE)
        x, c = d // 2, lax.rem(d, 2)
        sends = []

        def rcopy(src, dst, ssem, rsem, dev):
            cp = pltpu.make_async_remote_copy(src_ref=src, dst_ref=dst, send_sem=ssem, recv_sem=rsem,
                                              device_id=dev, device_id_type=MESH)
            cp.start()
            sends.append(cp)
            return cp

        class RingSum:
            def __init__(self, sl, buf, ss, rs, dev, p):
                self.sl, self.buf, self.ss, self.rs, self.dev = sl, buf, ss, rs, dev
                self.p, self.nxt, self.prv, self.opp = p, lax.rem(p + 1, SIDE), lax.rem(p + 3, SIDE), lax.rem(p + 2, SIDE)

            def send(self, k, q, half, to):
                return rcopy(self.sl(q, half), self.buf(k), self.ss.at[k], self.rs.at[k], self.dev(to))

            def start(self):
                self.a0 = self.send(0, self.opp, 0, self.nxt)
                self.a1 = self.send(1, self.opp, 1, self.prv)
                self.b0 = self.send(2, self.nxt, 1, self.nxt)
                self.b1 = self.send(3, self.prv, 0, self.prv)

            def mid(self):
                self.a0.wait_recv()
                part = self.sl(self.nxt, 0)
                part[...] += self.buf(0)[...]
                self.c0 = self.send(4, self.nxt, 0, self.nxt)
                self.a1.wait_recv()
                part = self.sl(self.prv, 1)
                part[...] += self.buf(1)[...]
                self.c1 = self.send(5, self.prv, 1, self.prv)

            def end(self):
                for cp in (self.b0, self.b1, self.c0, self.c1):
                    cp.wait_recv()
                return (self.sl(self.p, 0)[...] + self.buf(4)[...] + self.buf(3)[...],
                        self.sl(self.p, 1)[...] + self.buf(2)[...] + self.buf(5)[...])

        class RingGather:
            def __init__(self, sl, ss, rs, dev, p):
                self.sl, self.ss, self.rs, self.dev = sl, ss, rs, dev
                self.p, self.nxt, self.prv = p, lax.rem(p + 1, SIDE), lax.rem(p + 3, SIDE)

            def send(self, k, q, half, to):
                return rcopy(self.sl(q, half), self.sl(q, half), self.ss.at[k], self.rs.at[k], self.dev(to))

            def start(self):
                self.a0 = self.send(0, self.p, 0, self.nxt)
                self.a1 = self.send(1, self.p, 1, self.prv)
                self.b0 = self.send(2, self.p, 1, self.nxt)
                self.b1 = self.send(3, self.p, 0, self.prv)

            def mid(self):
                self.a0.wait_recv()
                self.c0 = self.send(4, self.prv, 0, self.nxt)
                self.a1.wait_recv()
                self.c1 = self.send(5, self.nxt, 1, self.prv)

            def end(self):
                for cp in (self.b0, self.b1, self.c0, self.c1):
                    cp.wait_recv()

        in_cp = [pltpu.make_async_copy(e_hbm, et, in_sem.at[0])]
        for h in range(2):
            rows = pl.ds(h * ht, ht)
            in_cp.append(pltpu.make_async_copy(t_hbm.at[rows, :], t_v.at[rows, :], in_sem.at[1 + h]))
        for cp in (in_cp[1], in_cp[0], in_cp[2]):
            cp.start()

        barrier = pltpu.get_barrier_semaphore()
        for k in range(1, nt):
            pl.semaphore_signal(barrier, inc=1, device_id={'tp': lax.rem(t + k, nt), 'dp': d}, device_id_type=MESH)
        for k in range(1, nd):
            pl.semaphore_signal(barrier, inc=1, device_id={'tp': t, 'dp': lax.rem(d + k, nd)}, device_id_type=MESH)

        def pad_f(a, axis):
            shape = list(a.shape)
            shape[axis] = dpad - dim
            return jnp.concatenate([a, jnp.zeros(shape, F32)], axis=axis) if dpad > dim else a

        wrow = pad_f(1.0 + w_ref[...].astype(F32).reshape(1, dim), 1)
        wpc[...] = jnp.broadcast_to(wrow, (128, dpad)).T[:dim, :]

        def norm_step(i, _):
            r0 = pl.multiple_of(i * 128, 128)
            xv = hid[:, pl.ds(r0, 128)].astype(F32)
            s = lax.rsqrt(jnp.mean(xv * xv, axis=0, keepdims=True) + EPS)
            g = xv * s * wpc[...]
            gb[pl.ds(r0, 128), :] = pad_f(g, 0).T[:, :dim].astype(BF16)
            gp = [g[(2 * xx + cc) * cols:(2 * xx + cc + 1) * cols, :] for cc in range(2) for xx in range(SIDE)]
            gt[:, pl.ds(r0, 128)] = jnp.concatenate(gp, axis=0).astype(BF16)
            return 0

        lax.fori_loop(0, tok // 128, norm_step, 0)

        maskf = mask_ref[...].astype(F32)
        mk_s[...] = jnp.broadcast_to(jnp.sum(maskf, axis=1, keepdims=True), (8, 128))
        mk_r[d] = mk_s[...]
        pl.semaphore_wait(barrier, nt + nd - 2)
        mk_cp = [rcopy(mk_s, mk_r.at[d], ss_mk.at[k], rs_mk.at[k], {'tp': t, 'dp': lax.rem(d + k, nd)}) for k in range(1, nd)]

        def forward(h):
            base = h * ht
            in_cp[1 + h].wait()

            def mx(i, _):
                r = pl.multiple_of(base + i * 64, 64)
                m = t_v[pl.ds(r, 64), 0:128]
                for q in range(1, voc // 128):
                    m = jnp.maximum(m, t_v[pl.ds(r, 64), q * 128:(q + 1) * 128])
                mm = jnp.max(m.astype(F32), axis=1, keepdims=True)
                mcol[h, pl.ds(pl.multiple_of(i * 64, 64), 64), :] = jnp.broadcast_to(mm, (64, 128))
                return 0

            lax.fori_loop(0, ht // 64, mx, 0)
            if h == 0:
                in_cp[0].wait()
            acc[...] = jnp.zeros_like(acc)

            def fdot(b, slot):
                v0 = pl.multiple_of(b * vb, vb)
                scr[slot] = jnp.dot(gb[base:base + ht, :], et[:, pl.ds(v0, vb)], preferred_element_type=F32)

            def elem(b, slot):
                for i in range(0, ht, 32):
                    r = slice(base + i, base + i + 32)
                    a = slice(i, i + 32)
                    m = mcol[h, a, :]
                    zs, zt, qs = acc[0, a, :], acc[1, a, :], acc[2, a, :]
                    for q in range(vb // 128):
                        lanes = pl.ds(pl.multiple_of(b * vb + q * 128, 128), 128)
                        th = jnp.tanh(scr[slot, a, q * 128:(q + 1) * 128] * (1.0 / CAP))
                        tv[r, lanes] = th
                        u = t_v[r, lanes].astype(F32) - m
                        ex = jnp.exp2(u * LOG2E)
                        tx[r, lanes] = ex
                        zs = zs + jnp.exp2(th * (CAP * LOG2E))
                        zt = zt + ex
                        qs = qs + ex * (u - CAP * th)
                    acc[0, a, :] = zs
                    acc[1, a, :] = zt
                    acc[2, a, :] = qs

            fdot(0, 0)

            def vstep(i, _):
                b = i * 2
                fdot(b + 1, 1)
                elem(b, 0)
                fdot(jnp.minimum(b + 2, nvb - 1), 0)
                elem(b + 1, 1)
                return 0

            lax.fori_loop(0, nvb // 2, vstep, 0)
            parts = [mcol[h].T[0:1, :]] + [jnp.sum(acc[k].T, axis=0, keepdims=True) for k in range(3)]
            st_s[h] = jnp.concatenate(parts + [jnp.zeros((4, ht), F32)], axis=0)
            st_r[h, t] = st_s[h]
            return [rcopy(st_s.at[h], st_r.at[h, t], ss_st.at[h, k], rs_st.at[h, k], {'tp': lax.rem(t + k, nt), 'dp': d})
                    for k in range(1, nt)]

        def combine(h, cps, inv_m):
            for cp in cps:
                cp.wait_recv()
            mts = st_r[h, :, 0, :]
            mt = jnp.max(mts, axis=0, keepdims=True)
            dm = jnp.maximum(mts - mt, -3e38)
            e = jnp.exp(dm)
            zte = st_r[h, :, 2, :] * e
            zt = jnp.sum(zte, axis=0, keepdims=True)
            zs = jnp.sum(st_r[h, :, 1, :], axis=0, keepdims=True)
            a = jnp.sum(st_r[h, :, 3, :] * e + zte * dm, axis=0, keepdims=True)
            kl = a / zt - jnp.log(zt) + jnp.log(zs)
            w = maskf[:, h * ht:(h + 1) * ht] * inv_m
            mine = jnp.exp(jnp.maximum(st_s[h, 0:1, :] - mt, -3e38))
            for k, row in enumerate((w / zs, w / zt * mine)):
                col[k, h * ht:(h + 1) * ht, :] = jnp.broadcast_to(row, (128, ht)).T
            return jnp.sum(w * kl, axis=1, keepdims=True)

        def dlogit(h):
            base = h * ht

            def rstep(i, _):
                r = pl.ds(pl.multiple_of(base + i * 16, 16), 16)
                cs, ct = col[0, r, :], col[1, r, :]
                for q in range(voc // 128):
                    lanes = slice(q * 128, (q + 1) * 128)
                    th = tv[r, lanes]
                    ps = jnp.exp2(th * (CAP * LOG2E)) * cs
                    t_v[r, lanes] = ((ps - tx[r, lanes] * ct) * (1.0 - th * th)).astype(BF16)
                return 0

            lax.fori_loop(0, ht // 16, rstep, 0)

        def dgrad(h):
            rows = slice(h * ht, (h + 1) * ht)
            dg[:, rows] = lax.dot_general(et[...], t_v[rows, :], (((1,), (1,)), ((), ())), preferred_element_type=F32)

        pos1, pos2 = (z, y), (y, z)

        def chunk(h, q):
            return pl.ds(pl.multiple_of(h * ht + q * zc, zc), zc)

        def frows(q, half):
            return pl.ds(pl.multiple_of(q * fp + half * (fp // 2), 8), fp // 2)

        def dev1(h):
            return lambda q: {'tp': q * SIDE + y if h == 0 else z * SIDE + q, 'dp': d}

        def dev2(h):
            return lambda q: {'tp': z * SIDE + q if h == 0 else q * SIDE + y, 'dp': d}

        def make(h):
            r1 = RingSum(lambda q, half: dg.at[half * half_d:(half + 1) * half_d, chunk(h, q)], lambda k: zr.at[h, k],
                         ss_z.at[h], rs_z.at[h], dev1(h), pos1[h])
            r2 = RingSum(lambda q, half: dg.at[frows(q, half), chunk(h, pos1[h])], lambda k: p2r.at[h, k],
                         ss_p.at[h], rs_p.at[h], dev2(h), pos2[h])
            g1 = RingGather(lambda q, half: agb.at[h, frows(q, half), :], ss_g.at[h], rs_g.at[h], dev2(h), pos2[h])
            g2 = RingGather(lambda q, half: dhf.at[half * half_d:(half + 1) * half_d, chunk(h, q)],
                            ss_h.at[h], rs_h.at[h], dev1(h), pos1[h])
            return r1, r2, g1, g2

        ring = (make(0), make(1))

        def rs_end(h):
            r1, r2 = ring[h][:2]
            lo_v, hi_v = r1.end()
            r1.sl(r1.p, 0)[...] = lo_v
            r1.sl(r1.p, 1)[...] = hi_v
            r2.start()

        def p2_end(h):
            r2, g1 = ring[h][1:3]
            lo_v, hi_v = r2.end()
            g1.sl(g1.p, 0)[...] = lo_v
            g1.sl(g1.p, 1)[...] = hi_v
            g1.start()

        def norm_back(h):
            g1, g2 = ring[h][2:]
            g1.end()
            ck = chunk(h, pos1[h])
            gv = agb[h]
            xv = hid[:, ck].astype(F32)
            s = lax.rsqrt(jnp.mean(xv * xv, axis=0, keepdims=True) + EPS)
            cv = gv * wpc[:, :zc]
            m = jnp.mean(cv * xv, axis=0, keepdims=True)
            dhf[:, ck] = s * cv - xv * (s * s * s * m)
            g2.start()
            return gv * xv * s

        def ag_end(h):
            ring[h][3].end()
            rows = slice(h * ht, (h + 1) * ht)
            dh_out[:, rows] = dhf[:, rows].astype(BF16)

        def de_start(j):
            tv[0:dim, j * vc:(j + 1) * vc] = jnp.dot(gt[...], t_v[:, j * vc:(j + 1) * vc], preferred_element_type=F32)
            other = pl.ds(pl.multiple_of((1 - c) * half_d, 8), half_d)
            return rcopy(tv.at[other, j * vc:(j + 1) * vc], d2r.at[j], ss_d.at[j], rs_d.at[j], {'tp': t, 'dp': x * 2 + 1 - c})

        def make_x(j):
            def sl(q, half):
                return tv.at[pl.ds(pl.multiple_of(c * half_d + q * cols, 8), cols), j * vc + half * vh:j * vc + (half + 1) * vh]

            return RingSum(sl, lambda k: xr.at[j, k], ss_x.at[j], rs_x.at[j], lambda q: {'tp': t, 'dp': q * 2 + c}, x)

        xring = [make_x(j) for j in range(NV)]

        def x_start(j, cp):
            cp.wait_recv()
            mine = pl.ds(pl.multiple_of(c * half_d, 8), half_d)
            tv[mine, j * vc:(j + 1) * vc] += d2r[j]
            xring[j].start()

        def x_end(j):
            lo_v, hi_v = xring[j].end()
            det_out[:, j * vc:j * vc + vh] = lo_v
            det_out[:, j * vc + vh:(j + 1) * vc] = hi_v

        st0 = forward(0)
        st1 = forward(1)
        for cp in mk_cp:
            cp.wait_recv()
        inv_m = 1.0 / jnp.sum(mk_r[:, 0, :], axis=0, keepdims=True)[:, 0:1]
        loss = combine(0, st0, inv_m)
        dlogit(0)
        dgrad(0)
        ring[0][0].start()
        loss = loss + combine(1, st1, inv_m)
        dlogit(1)
        dd = [None] * NV
        dd[0] = de_start(0)
        dgrad(1)
        ring[1][0].start()
        x_start(0, dd[0])
        dd[1] = de_start(1)
        ring[0][0].mid()
        dd[2] = de_start(2)
        x_start(1, dd[1])
        dd[3] = de_start(3)
        x_start(2, dd[2])
        ring[1][0].mid()
        x_start(3, dd[3])
        xring[0].mid()
        rs_end(0)
        xring[1].mid()
        rs_end(1)
        ring[0][1].mid()
        ring[1][1].mid()
        xring[2].mid()
        p2_end(0)
        p2_end(1)
        ring[0][2].mid()
        ring[1][2].mid()
        xring[3].mid()
        p0 = norm_back(0)
        p1 = norm_back(1)
        pw = jnp.where(y == 0, p0, 0.0) + jnp.where(z == 0, p1, 0.0)
        dwv = jnp.sum(pad_f(pw, 0).T, axis=0, keepdims=True)
        dwt_s[...] = jnp.zeros((8, 128), F32)
        for k in range(dpad // 128):
            dwt_s[k:k + 1, :] = dwv[:, k * 128:(k + 1) * 128]
        dwt_r[t] = dwt_s[...]
        wt = [rcopy(dwt_s, dwt_r.at[t], ss_wt.at[k], rs_wt.at[k], {'tp': lax.rem(t + k, nt), 'dp': d}) for k in range(1, nt)]
        ring[0][3].mid()
        ring[1][3].mid()
        x_end(0)
        for cp in wt:
            cp.wait_recv()
        dws = jnp.sum(dwt_r[...], axis=0)
        rowi = lax.broadcasted_iota(jnp.int32, (8, 128), 0)
        dwd_s[...] = jnp.where(rowi == 7, jnp.broadcast_to(loss, (8, 128)), dws)
        dwd_r[d] = dwd_s[...]
        wd = [rcopy(dwd_s, dwd_r.at[d], ss_wd.at[k], rs_wd.at[k], {'tp': t, 'dp': lax.rem(d + k, nd)}) for k in range(1, nd)]
        x_end(1)
        x_end(2)
        x_end(3)
        ag_end(0)
        ag_end(1)
        for cp in wd:
            cp.wait_recv()
        dwf = jnp.sum(dwd_r[...], axis=0)
        loss_out[...] = dwf[7:8, 0:1]
        for k in range(dpad // 128):
            n = min(128, dim - k * 128)
            dw_out[:, k * 128:k * 128 + n] = dwf[k:k + 1, 0:n]
        for cp in sends:
            cp.wait_send()

    sem = pltpu.SemaphoreType.DMA
    vmem = pltpu.VMEM
    scratch = [
        vmem((dim, voc), BF16), vmem((tok, voc), BF16), vmem((tok, dim), BF16), vmem((dim, tok), BF16),
        vmem((tok, voc), F32), vmem((tok, voc), F32), vmem((2, ht, vb), F32), vmem((dim, 128), F32),
        vmem((dim, tok), F32), vmem((dim, tok), F32),
        vmem((3, ht, 128), F32), vmem((2, ht, 128), F32), vmem((2, tok, 128), F32),
        vmem((2, 8, ht), F32), vmem((2, nt, 8, ht), F32), vmem((8, 128), F32), vmem((nd, 8, 128), F32),
        vmem((8, 128), F32), vmem((nt, 8, 128), F32), vmem((8, 128), F32), vmem((nd, 8, 128), F32),
        vmem((2, 6, half_d, zc), F32), vmem((2, 6, fp // 2, zc), F32), vmem((2, dim, zc), F32),
        vmem((NV, half_d, vc), F32), vmem((NV, 6, cols, vh), F32),
        sem((3,)), sem((2, nt)), sem((2, nt)), sem((nd,)), sem((nd,)), sem((2, 6)), sem((2, 6)), sem((2, 6)), sem((2, 6)),
        sem((2, 6)), sem((2, 6)), sem((2, 6)), sem((2, 6)), sem((NV,)), sem((NV,)), sem((NV, 6)), sem((NV, 6)),
        sem((nt,)), sem((nt,)), sem((nd,)), sem((nd,)),
    ]
    vm = pl.BlockSpec(memory_space=pltpu.VMEM)
    anys = pl.BlockSpec(memory_space=pl.ANY)
    return pl.pallas_call(
        kernel,
        out_shape=(jax.ShapeDtypeStruct((1, 1), F32), jax.ShapeDtypeStruct((dim, tok), BF16),
                   jax.ShapeDtypeStruct((cols, voc), F32), jax.ShapeDtypeStruct((1, dim), F32)),
        in_specs=[vm, vm, vm, anys, anys],
        out_specs=(vm, vm, vm, vm),
        scratch_shapes=scratch,
        compiler_params=pltpu.CompilerParams(collective_id=0, has_side_effects=True, vmem_limit_bytes=67043328),
        name='head',
    )


def solution(mesh):
    nt, nd = mesh.shape['tp'], mesh.shape['dp']

    def device_fn(hid, norm_w, emb, teach, mask):
        tok, dim = hid.shape
        call = build(tok, dim, emb.shape[0], nt, nd)
        loss, dh, det, dw = call(hid.T, norm_w, mask.reshape(1, tok), emb.T, teach)
        return loss.reshape(()), dh.T, det.T, dw.reshape(dim)

    return jax.shard_map(device_fn, mesh=mesh, in_specs=(P('dp', None), P(None), P('tp', None), P('dp', 'tp'), P('dp')),
                         out_specs=(P(), P('dp', None), P('tp', 'dp'), P(None)), check_vma=False)
```

time: 303 us -> 86.9 us (0.29)
  blocking collectives: 121 us -> 0 us
  waiting for transfers between devices: 96.9 us -> 0 us
  Pallas kernels: 0 us -> 79.7 us
  other arithmetic: 39.2 us -> 1.28 us
  matrix products: 25.4 us -> 0 us
  between operations: 15.6 us -> 2.35 us
    psum x1 -> x0, waiting for transfers between devices: 96.9 us -> none  [device_fn(): lax.psum(jnp.dot(d_raw, emb_loc, preferred_element_type=jnp.float32), 'tp')]
    psum x3 -> x0, blocking collectives: 84.6 us -> none  [the longest x1 56.1 us: device_fn(): totals = lax.psum(local_sums, 'tp')]
    pallas_call x0 -> x1, Pallas kernels: none -> 79.7 us  [device_fn(): loss, dh, det, dw = call(hid.T, norm_w, mask.reshape(1, tok), emb.T, teach)]
    pmax x1 -> x0, blocking collectives: 36.1 us -> none  [device_fn(): lax.pmax(jnp.stack([jnp.max(capped, axis=-1), jnp.max(teach_f32, axis=-1)...]
    dot_general x3 -> x0, matrix products: 25.4 us -> none  [the longest x1 10.2 us: device_fn(): jnp.einsum('nd,vd->nv', normed, emb_loc, preferred_element_type=jnp.float32)]
    reduce_sum x5 -> x0, other arithmetic: 19.9 us -> none  [the longest x1 11.6 us: device_fn(): jnp.sum(stu_exp, axis=-1)]
    convert_element_type x2 -> x0, other arithmetic: 14.9 us -> none  [the longest x1 11.3 us: device_fn(): (prob_diff * weight[:, None] * (1.0 - tanh_val * tanh_val)).astype(jnp.bf...]
    reduce_max x2 -> x0, other arithmetic: 3.69 us -> none  [device_fn(): jnp.max(teach_f32, axis=-1)]
  transfers between devices with their start and end apart: 2 -> 0, of which waited for: 1 -> 0; matrix products, arithmetic and copies ran while one was open for 6% -> 0% of each run, Pallas kernels for 0% -> 0%
where the time goes in v2:
time: 86.9 us; the launch traced here: 86.7 us
  Pallas kernels  79.7 us (92%)
  local copies, waits for them, and re-layouts  3.36 us (4%)
  between operations  2.35 us (3%)
  other arithmetic  1.28 us (1%)
    pallas_call x1, Pallas kernels, device_fn(): loss, dh, det, dw = call(hid.T, norm_w, mask.reshape(1, tok), emb.T, teach)  79.7 us
    unnamed x4, local copies, waits for them, and re-layouts  3.36 us

profile of v2, /device:TPU:1, one launch (start us, length us, event | category | flops | bytes accessed | tf_op | source)
XLA Modules:
  0.0 86.7 jit_solution(11778492117880574519)
XLA Ops:
  0.6 79.7 %head.1 = (f32[1,1]{1,0:T(1,128)}, bf16[576,1024]{1,0:T(8,128)(2,1)}, f32[72,3072]{1,0:T(8,128)}, f32[1,576]{1,0:T(1,128)}) custom-call(bf16[576,1024]{1,0:T(8,128)(2,1)} %bitcast.8, bf16[576]{0:T(1024)(128)(2,1)} %w_ref.1, s32[1,1024]{1,0:T(1,128)} %bitcast.10, bf16[576,3072]{1,0:T(8,128)(2,1)} %bitcast.6, bf16[1024,3072]{1,0:T(8,128)(2,1)} %t_hbm.1), custom_call_target="tpu_custom_call" | custom-call | tf_op jit(solution)/shard_map/head/pallas_call | solution.py:424
  80.3 1.3 %reduce = f32[576]{0:T(1024)} reduce(f32[1,576]{1,0:T(1,128)} %get-tuple-element.11, f32[]{:T(128)} %constant), dimensions={0}, to_apply=%get-tuple-element.11.reduce_sub_computation | reduce | bytes 4612 | tf_op jit(solution)/shard_map/head/pallas_call | solution.py:424
  82.2 0.0 copy-start
  82.2 2.4 %copy.13 = bf16[1024,576]{0,1:T(8,128)(2,1)} copy(bf16[1024,576]{0,1:T(8,128)(2,1)} %bitcast.7) | data formatting | bytes 2359296
  84.6 0.0 copy-done
  84.6 0.9 %copy.14 = f32[3072,72]{0,1:T(8,128)} copy(f32[3072,72]{0,1:T(8,128)S(1)} %bitcast.9) | data formatting | bytes 1769472
Async XLA Ops:
  82.2 2.5 %copy-start = (f32[72,3072]{1,0:T(8,128)S(1)}, f32[72,3072]{1,0:T(8,128)}, u32[]{:S(2)}) copy-start(f32[72,3072]{1,0:T(8,128)} %get-tuple-element.10) | copy-start | bytes 2654212

commit v3 on v2

--- a/solution.py
+++ b/solution.py
@@ -8,11 +8,12 @@
 CAP = 30.0
 EPS = 1e-6
 LOG2E = 1.4426950408889634
+LN2 = 0.6931471805599453
 MESH = pl.DeviceIdType.MESH
 F32 = jnp.float32
 BF16 = jnp.bfloat16
 SIDE = 4
-NV = 4
+NV = 6
 
 
 def build(tok, dim, voc, nt, nd):
@@ -22,21 +23,22 @@
     cols = dim // nd
     vc = voc // NV
     vh = vc // 2
-    vb = 256
+    vb = min(512, voc // 2)
     nvb = voc // vb
     half_d = dim // 2
     dpad = -(-dim // 128) * 128
 
     def kernel(hid, w_ref, mask_ref, e_hbm, t_hbm, loss_out, dh_out, det_out, dw_out,
-               et, t_v, gb, gt, tv, tx, scr, wpc, dg, dhf, acc, mcol, col, st_s, st_r, mk_s, mk_r, dwt_s, dwt_r, dwd_s, dwd_r,
+               et, t_v, gb, gt, tv, tx, scr, wpc, dg, dhf, acc, mcol, col, st_s, st_r, mk_s, mk_r, dwa_s, dwa_r, dwd_s, dwd_r, dhb, deb,
                zr, p2r, agb, d2r, xr,
                in_sem, ss_st, rs_st, ss_mk, rs_mk, ss_z, rs_z, ss_p, rs_p, ss_g, rs_g, ss_h, rs_h,
-               ss_d, rs_d, ss_x, rs_x, ss_wt, rs_wt, ss_wd, rs_wd):
+               ss_d, rs_d, ss_x, rs_x, ss_wa, rs_wa, ss_wd, rs_wd, out_sem):
         t = lax.axis_index('tp')
         d = lax.axis_index('dp')
         z, y = t // SIDE, lax.rem(t, SIDE)
         x, c = d // 2, lax.rem(d, 2)
         sends = []
+        outs = []
 
         def rcopy(src, dst, ssem, rsem, dev):
             cp = pltpu.make_async_remote_copy(src_ref=src, dst_ref=dst, send_sem=ssem, recv_sem=rsem,
@@ -135,8 +137,6 @@
         maskf = mask_ref[...].astype(F32)
         mk_s[...] = jnp.broadcast_to(jnp.sum(maskf, axis=1, keepdims=True), (8, 128))
         mk_r[d] = mk_s[...]
-        pl.semaphore_wait(barrier, nt + nd - 2)
-        mk_cp = [rcopy(mk_s, mk_r.at[d], ss_mk.at[k], rs_mk.at[k], {'tp': t, 'dp': lax.rem(d + k, nd)}) for k in range(1, nd)]
 
         def forward(h):
             base = h * ht
@@ -161,21 +161,22 @@
                 scr[slot] = jnp.dot(gb[base:base + ht, :], et[:, pl.ds(v0, vb)], preferred_element_type=F32)
 
             def elem(b, slot):
-                for i in range(0, ht, 32):
-                    r = slice(base + i, base + i + 32)
-                    a = slice(i, i + 32)
+                for i in range(0, ht, 16):
+                    r = slice(base + i, base + i + 16)
+                    a = slice(i, i + 16)
                     m = mcol[h, a, :]
                     zs, zt, qs = acc[0, a, :], acc[1, a, :], acc[2, a, :]
                     for q in range(vb // 128):
                         lanes = pl.ds(pl.multiple_of(b * vb + q * 128, 128), 128)
                         th = jnp.tanh(scr[slot, a, q * 128:(q + 1) * 128] * (1.0 / CAP))
                         tv[r, lanes] = th
-                        u = t_v[r, lanes].astype(F32) - m
-                        ex = jnp.exp2(u * LOG2E)
+                        u = (t_v[r, lanes].astype(F32) - m) * LOG2E
+                        v = th * (CAP * LOG2E)
+                        ex = jnp.exp2(u)
                         tx[r, lanes] = ex
-                        zs = zs + jnp.exp2(th * (CAP * LOG2E))
+                        zs = zs + jnp.exp2(v)
                         zt = zt + ex
-                        qs = qs + ex * (u - CAP * th)
+                        qs = qs + ex * (u - v)
                     acc[0, a, :] = zs
                     acc[1, a, :] = zt
                     acc[2, a, :] = qs
@@ -194,6 +195,8 @@
             parts = [mcol[h].T[0:1, :]] + [jnp.sum(acc[k].T, axis=0, keepdims=True) for k in range(3)]
             st_s[h] = jnp.concatenate(parts + [jnp.zeros((4, ht), F32)], axis=0)
             st_r[h, t] = st_s[h]
+            if h == 0:
+                pl.semaphore_wait(barrier, nt + nd - 2)
             return [rcopy(st_s.at[h], st_r.at[h, t], ss_st.at[h, k], rs_st.at[h, k], {'tp': lax.rem(t + k, nt), 'dp': d})
                     for k in range(1, nt)]
 
@@ -207,7 +210,7 @@
             zte = st_r[h, :, 2, :] * e
             zt = jnp.sum(zte, axis=0, keepdims=True)
             zs = jnp.sum(st_r[h, :, 1, :], axis=0, keepdims=True)
-            a = jnp.sum(st_r[h, :, 3, :] * e + zte * dm, axis=0, keepdims=True)
+            a = jnp.sum(st_r[h, :, 3, :] * LN2 * e + zte * dm, axis=0, keepdims=True)
             kl = a / zt - jnp.log(zt) + jnp.log(zs)
             w = maskf[:, h * ht:(h + 1) * ht] * inv_m
             mine = jnp.exp(jnp.maximum(st_s[h, 0:1, :] - mt, -3e38))
@@ -283,14 +286,24 @@
             s = lax.rsqrt(jnp.mean(xv * xv, axis=0, keepdims=True) + EPS)
             cv = gv * wpc[:, :zc]
             m = jnp.mean(cv * xv, axis=0, keepdims=True)
+            dwv = jnp.sum(pad_f(gv * xv * s, 0).T, axis=0, keepdims=True)
+            for k in range(8):
+                part = dwv[:, k * 128:(k + 1) * 128] if k < dpad // 128 else jnp.zeros((1, 128), F32)
+                dwa_s[h, k:k + 1, :] = part
+            dwa_r[h, pos1[h]] = dwa_s[h]
+            cps = [rcopy(dwa_s.at[h], dwa_r.at[h, pos1[h]], ss_wa.at[h, k], rs_wa.at[h, k], dev1(h)(lax.rem(pos1[h] + k, SIDE)))
+                   for k in range(1, SIDE)]
             dhf[:, ck] = s * cv - xv * (s * s * s * m)
             g2.start()
-            return gv * xv * s
+            return cps
 
         def ag_end(h):
             ring[h][3].end()
             rows = slice(h * ht, (h + 1) * ht)
-            dh_out[:, rows] = dhf[:, rows].astype(BF16)
+            dhb[:, rows] = dhf[:, rows].astype(BF16)
+            cp = pltpu.make_async_copy(dhb.at[:, rows], dh_out.at[:, rows], out_sem.at[h])
+            cp.start()
+            outs.append(cp)
 
         def de_start(j):
             tv[0:dim, j * vc:(j + 1) * vc] = jnp.dot(gt[...], t_v[:, j * vc:(j + 1) * vc], preferred_element_type=F32)
@@ -313,78 +326,151 @@
 
         def x_end(j):
             lo_v, hi_v = xring[j].end()
-            det_out[:, j * vc:j * vc + vh] = lo_v
-            det_out[:, j * vc + vh:(j + 1) * vc] = hi_v
-
-        st0 = forward(0)
-        st1 = forward(1)
-        for cp in mk_cp:
-            cp.wait_recv()
-        inv_m = 1.0 / jnp.sum(mk_r[:, 0, :], axis=0, keepdims=True)[:, 0:1]
-        loss = combine(0, st0, inv_m)
-        dlogit(0)
-        dgrad(0)
-        ring[0][0].start()
-        loss = loss + combine(1, st1, inv_m)
-        dlogit(1)
-        dd = [None] * NV
-        dd[0] = de_start(0)
-        dgrad(1)
-        ring[1][0].start()
-        x_start(0, dd[0])
-        dd[1] = de_start(1)
-        ring[0][0].mid()
-        dd[2] = de_start(2)
-        x_start(1, dd[1])
-        dd[3] = de_start(3)
-        x_start(2, dd[2])
-        ring[1][0].mid()
-        x_start(3, dd[3])
-        xring[0].mid()
-        rs_end(0)
-        xring[1].mid()
-        rs_end(1)
-        ring[0][1].mid()
-        ring[1][1].mid()
-        xring[2].mid()
-        p2_end(0)
-        p2_end(1)
-        ring[0][2].mid()
-        ring[1][2].mid()
-        xring[3].mid()
-        p0 = norm_back(0)
-        p1 = norm_back(1)
-        pw = jnp.where(y == 0, p0, 0.0) + jnp.where(z == 0, p1, 0.0)
-        dwv = jnp.sum(pad_f(pw, 0).T, axis=0, keepdims=True)
-        dwt_s[...] = jnp.zeros((8, 128), F32)
-        for k in range(dpad // 128):
-            dwt_s[k:k + 1, :] = dwv[:, k * 128:(k + 1) * 128]
-        dwt_r[t] = dwt_s[...]
-        wt = [rcopy(dwt_s, dwt_r.at[t], ss_wt.at[k], rs_wt.at[k], {'tp': lax.rem(t + k, nt), 'dp': d}) for k in range(1, nt)]
-        ring[0][3].mid()
-        ring[1][3].mid()
-        x_end(0)
-        for cp in wt:
-            cp.wait_recv()
-        dws = jnp.sum(dwt_r[...], axis=0)
-        rowi = lax.broadcasted_iota(jnp.int32, (8, 128), 0)
-        dwd_s[...] = jnp.where(rowi == 7, jnp.broadcast_to(loss, (8, 128)), dws)
-        dwd_r[d] = dwd_s[...]
-        wd = [rcopy(dwd_s, dwd_r.at[d], ss_wd.at[k], rs_wd.at[k], {'tp': t, 'dp': lax.rem(d + k, nd)}) for k in range(1, nd)]
-        x_end(1)
-        x_end(2)
-        x_end(3)
-        ag_end(0)
-        ag_end(1)
-        for cp in wd:
-            cp.wait_recv()
-        dwf = jnp.sum(dwd_r[...], axis=0)
-        loss_out[...] = dwf[7:8, 0:1]
-        for k in range(dpad // 128):
-            n = min(128, dim - k * 128)
-            dw_out[:, k * 128:k * 128 + n] = dwf[k:k + 1, 0:n]
-        for cp in sends:
-            cp.wait_send()
+            deb[:, j * vc:j * vc + vh] = lo_v
+            deb[:, j * vc + vh:(j + 1) * vc] = hi_v
+            cp = pltpu.make_async_copy(deb.at[:, j * vc:(j + 1) * vc], det_out.at[:, j * vc:(j + 1) * vc], out_sem.at[2 + j])
+            cp.start()
+            outs.append(cp)
+
+        with jax.named_scope('s00_st0_forward_0_'):
+            st0 = forward(0)
+        with jax.named_scope('s01_mk_cp_rcopy_mk_s_mk_r_at_d_s'):
+            mk_cp = [rcopy(mk_s, mk_r.at[d], ss_mk.at[k], rs_mk.at[k], {'tp': t, 'dp': lax.rem(d + k, nd)}) for k in range(1, nd)]
+        with jax.named_scope('s02_st1_forward_1_'):
+            st1 = forward(1)
+        with jax.named_scope('s03_for_cp_in_mk_cp_'):
+            for cp in mk_cp:
+                cp.wait_recv()
+        with jax.named_scope('s04_inv_m_1_0_jnp_sum_mk_r_0_axi'):
+            inv_m = 1.0 / jnp.sum(mk_r[:, 0, :], axis=0, keepdims=True)[:, 0:1]
+        with jax.named_scope('s05_loss_combine_0_st0_inv_m_'):
+            loss = combine(0, st0, inv_m)
+        with jax.named_scope('s06_dlogit_0_'):
+            dlogit(0)
+        with jax.named_scope('s07_dgrad_0_'):
+            dgrad(0)
+        with jax.named_scope('s08_ring_0_0_start_'):
+            ring[0][0].start()
+        with jax.named_scope('s09_loss_loss_combine_1_st1_inv_'):
+            loss = loss + combine(1, st1, inv_m)
+        with jax.named_scope('s10_dlogit_1_'):
+            dlogit(1)
+        with jax.named_scope('s11_dgrad_1_'):
+            dgrad(1)
+        with jax.named_scope('s12_ring_1_0_start_'):
+            ring[1][0].start()
+        with jax.named_scope('s13_dd_None_NV'):
+            dd = [None] * NV
+        with jax.named_scope('s14_dd_0_de_start_0_'):
+            dd[0] = de_start(0)
+        with jax.named_scope('s15_dd_1_de_start_1_'):
+            dd[1] = de_start(1)
+        with jax.named_scope('s16_ring_0_0_mid_'):
+            ring[0][0].mid()
+        with jax.named_scope('s17_dd_2_de_start_2_'):
+            dd[2] = de_start(2)
+        with jax.named_scope('s18_x_start_0_dd_0_'):
+            x_start(0, dd[0])
+        with jax.named_scope('s19_dd_3_de_start_3_'):
+            dd[3] = de_start(3)
+        with jax.named_scope('s20_x_start_1_dd_1_'):
+            x_start(1, dd[1])
+        with jax.named_scope('s21_dd_4_de_start_4_'):
+            dd[4] = de_start(4)
+        with jax.named_scope('s22_x_start_2_dd_2_'):
+            x_start(2, dd[2])
+        with jax.named_scope('s23_dd_5_de_start_5_'):
+            dd[5] = de_start(5)
+        with jax.named_scope('s24_x_start_3_dd_3_'):
+            x_start(3, dd[3])
+        with jax.named_scope('s25_x_start_4_dd_4_'):
+            x_start(4, dd[4])
+        with jax.named_scope('s26_ring_1_0_mid_'):
+            ring[1][0].mid()
+        with jax.named_scope('s27_x_start_5_dd_5_'):
+            x_start(5, dd[5])
+        with jax.named_scope('s28_xring_0_mid_'):
+            xring[0].mid()
+        with jax.named_scope('s29_rs_end_0_'):
+            rs_end(0)
+        with jax.named_scope('s30_xring_1_mid_'):
+            xring[1].mid()
+        with jax.named_scope('s31_ring_0_1_mid_'):
+            ring[0][1].mid()
+        with jax.named_scope('s32_rs_end_1_'):
+            rs_end(1)
+        with jax.named_scope('s33_xring_2_mid_'):
+            xring[2].mid()
+        with jax.named_scope('s34_p2_end_0_'):
+            p2_end(0)
+        with jax.named_scope('s35_ring_1_1_mid_'):
+            ring[1][1].mid()
+        with jax.named_scope('s36_xring_3_mid_'):
+            xring[3].mid()
+        with jax.named_scope('s37_ring_0_2_mid_'):
+            ring[0][2].mid()
+        with jax.named_scope('s38_p2_end_1_'):
+            p2_end(1)
+        with jax.named_scope('s39_xring_4_mid_'):
+            xring[4].mid()
+        with jax.named_scope('s40_wa0_norm_back_0_'):
+            wa0 = norm_back(0)
+        with jax.named_scope('s41_ring_1_2_mid_'):
+            ring[1][2].mid()
+        with jax.named_scope('s42_xring_5_mid_'):
+            xring[5].mid()
+        with jax.named_scope('s43_wa1_norm_back_1_'):
+            wa1 = norm_back(1)
+        with jax.named_scope('s44_ring_0_3_mid_'):
+            ring[0][3].mid()
+        with jax.named_scope('s45_for_cp_in_wa0_wa1_'):
+            for cp in wa0 + wa1:
+                cp.wait_recv()
+        with jax.named_scope('s46_dws_jnp_sum_dwa_r_0_axis_0_j'):
+            dws = jnp.sum(dwa_r[0], axis=0) + jnp.sum(dwa_r[1], axis=0)
+        with jax.named_scope('s47_rowi_lax_broadcasted_iota_jn'):
+            rowi = lax.broadcasted_iota(jnp.int32, (8, 128), 0)
+        with jax.named_scope('s48_dwd_s_jnp_where_rowi_7_jnp_b'):
+            dwd_s[...] = jnp.where(rowi == 7, jnp.broadcast_to(loss, (8, 128)), dws)
+        with jax.named_scope('s49_dwd_r_d_dwd_s_'):
+            dwd_r[d] = dwd_s[...]
+        with jax.named_scope('s50_wd_rcopy_dwd_s_dwd_r_at_d_ss'):
+            wd = [rcopy(dwd_s, dwd_r.at[d], ss_wd.at[k], rs_wd.at[k], {'tp': t, 'dp': lax.rem(d + k, nd)}) for k in range(1, nd)]
+        with jax.named_scope('s51_x_end_0_'):
+            x_end(0)
+        with jax.named_scope('s52_x_end_1_'):
+            x_end(1)
+        with jax.named_scope('s53_ring_1_3_mid_'):
+            ring[1][3].mid()
+        with jax.named_scope('s54_x_end_2_'):
+            x_end(2)
+        with jax.named_scope('s55_x_end_3_'):
+            x_end(3)
+        with jax.named_scope('s56_x_end_4_'):
+            x_end(4)
+        with jax.named_scope('s57_ag_end_0_'):
+            ag_end(0)
+        with jax.named_scope('s58_x_end_5_'):
+            x_end(5)
+        with jax.named_scope('s59_for_cp_in_wd_'):
+            for cp in wd:
+                cp.wait_recv()
+        with jax.named_scope('s60_dwf_jnp_sum_dwd_r_axis_0_'):
+            dwf = jnp.sum(dwd_r[...], axis=0)
+        with jax.named_scope('s61_loss_out_dwf_7_8_0_1_'):
+            loss_out[...] = dwf[7:8, 0:1]
+        with jax.named_scope('s62_for_k_in_range_dpad_128_'):
+            for k in range(dpad // 128):
+                n = min(128, dim - k * 128)
+                dw_out[:, k * 128:k * 128 + n] = dwf[k:k + 1, 0:n]
+        with jax.named_scope('s63_for_cp_in_sends_'):
+            for cp in sends:
+                cp.wait_send()
+        with jax.named_scope('s64_ag_end_1_'):
+            ag_end(1)
+        with jax.named_scope('s65_for_cp_in_outs_'):
+            for cp in outs:
+                cp.wait()
 
     sem = pltpu.SemaphoreType.DMA
     vmem = pltpu.VMEM
@@ -394,12 +480,13 @@
         vmem((dim, tok), F32), vmem((dim, tok), F32),
         vmem((3, ht, 128), F32), vmem((2, ht, 128), F32), vmem((2, tok, 128), F32),
         vmem((2, 8, ht), F32), vmem((2, nt, 8, ht), F32), vmem((8, 128), F32), vmem((nd, 8, 128), F32),
-        vmem((8, 128), F32), vmem((nt, 8, 128), F32), vmem((8, 128), F32), vmem((nd, 8, 128), F32),
+        vmem((2, 8, 128), F32), vmem((2, SIDE, 8, 128), F32), vmem((8, 128), F32), vmem((nd, 8, 128), F32),
+        vmem((dim, tok), BF16), vmem((cols, voc), F32),
         vmem((2, 6, half_d, zc), F32), vmem((2, 6, fp // 2, zc), F32), vmem((2, dim, zc), F32),
         vmem((NV, half_d, vc), F32), vmem((NV, 6, cols, vh), F32),
         sem((3,)), sem((2, nt)), sem((2, nt)), sem((nd,)), sem((nd,)), sem((2, 6)), sem((2, 6)), sem((2, 6)), sem((2, 6)),
         sem((2, 6)), sem((2, 6)), sem((2, 6)), sem((2, 6)), sem((NV,)), sem((NV,)), sem((NV, 6)), sem((NV, 6)),
-        sem((nt,)), sem((nt,)), sem((nd,)), sem((nd,)),
+        sem((2, SIDE)), sem((2, SIDE)), sem((nd,)), sem((nd,)), sem((2 + NV,)),
     ]
     vm = pl.BlockSpec(memory_space=pltpu.VMEM)
     anys = pl.BlockSpec(memory_space=pl.ANY)
@@ -408,13 +495,48 @@
         out_shape=(jax.ShapeDtypeStruct((1, 1), F32), jax.ShapeDtypeStruct((dim, tok), BF16),
                    jax.ShapeDtypeStruct((cols, voc), F32), jax.ShapeDtypeStruct((1, dim), F32)),
         in_specs=[vm, vm, vm, anys, anys],
-        out_specs=(vm, vm, vm, vm),
+        out_specs=(vm, anys, anys, vm),
         scratch_shapes=scratch,
         compiler_params=pltpu.CompilerParams(collective_id=0, has_side_effects=True, vmem_limit_bytes=67043328),
         name='head',
     )
 
 
+def finish(tok, dim, voc, cols):
+    parts = 4
+    rb, lb = tok // parts, voc // parts
+
+    def kernel(dh, det, dw, dh_o, det_o, dw_o, hb, eb, sem_i, sem_o):
+        views = []
+        for i in range(parts):
+            ls, es = pl.ds(i * rb, rb), pl.ds(i * lb, lb)
+            views.append((dh.at[:, ls], hb.at[:, ls], dh_o.at[:, ls]))
+            views.append((det.at[:, es], eb.at[:, es], det_o.at[:, es]))
+        ins = [pltpu.make_async_copy(a, b, sem_i.at[k]) for k, (a, b, _) in enumerate(views)]
+        outs = [pltpu.make_async_copy(b, o, sem_o.at[k]) for k, (_, b, o) in enumerate(views)]
+        for cp in ins:
+            cp.start()
+        dw_o[...] = dw[...].reshape(dim)
+        for ci, co in zip(ins, outs):
+            ci.wait()
+            co.start()
+        for co in outs:
+            co.wait()
+
+    vm = pl.BlockSpec(memory_space=pltpu.VMEM)
+    anys = pl.BlockSpec(memory_space=pl.ANY)
+    return pl.pallas_call(
+        kernel,
+        out_shape=(jax.ShapeDtypeStruct((dim, tok), BF16), jax.ShapeDtypeStruct((cols, voc), F32), jax.ShapeDtypeStruct((dim,), F32)),
+        in_specs=[anys, anys, vm],
+        out_specs=(anys, anys, vm),
+        scratch_shapes=[pltpu.VMEM((dim, tok), BF16), pltpu.VMEM((cols, voc), F32),
+                        pltpu.SemaphoreType.DMA((2 * parts,)), pltpu.SemaphoreType.DMA((2 * parts,))],
+        compiler_params=pltpu.CompilerParams(vmem_limit_bytes=67043328),
+        name='finish',
+    )
+
+
 def solution(mesh):
     nt, nd = mesh.shape['tp'], mesh.shape['dp']
 
@@ -422,7 +544,8 @@
         tok, dim = hid.shape
         call = build(tok, dim, emb.shape[0], nt, nd)
         loss, dh, det, dw = call(hid.T, norm_w, mask.reshape(1, tok), emb.T, teach)
-        return loss.reshape(()), dh.T, det.T, dw.reshape(dim)
+        dh, det, dw = finish(tok, dim, emb.shape[0], dim // nd)(dh, det, dw)
+        return loss.reshape(()), dh.T, det.T, dw
 
     return jax.shard_map(device_fn, mesh=mesh, in_specs=(P('dp', None), P(None), P('tp', None), P('dp', 'tp'), P('dp')),
                          out_specs=(P(), P('dp', None), P('tp', 'dp'), P(None)), check_vma=False)

time: 86.9 us -> 83.3 us (0.959)
  local copies, waits for them, and re-layouts: 3.36 us -> 0 us
  other arithmetic: 1.28 us -> 0 us
    pallas_call x0 -> x1, Pallas kernels: none -> 3.69 us  [device_fn(): dh, det, dw = finish(tok, dim, emb.shape[0], dim // nd)(dh, det, dw)]
    unnamed x4 -> x0, local copies, waits for them, and re-layouts: 3.36 us -> none
    pallas_call x1, Pallas kernels: 79.7 us -> 76.5 us  [device_fn(): loss, dh, det, dw = call(hid.T, norm_w, mask.reshape(1, tok), emb.T, teach)]
    pallas_call x1 -> x0, other arithmetic: 1.28 us -> none  [device_fn(): loss, dh, det, dw = call(hid.T, norm_w, mask.reshape(1, tok), emb.T, teach)]
where the time goes in v3:
time: 83.3 us; the launch traced here: 82.5 us
  Pallas kernels  80.1 us (96%)
  between operations  2.38 us (3%)
    pallas_call x1, Pallas kernels, device_fn(): loss, dh, det, dw = call(hid.T, norm_w, mask.reshape(1, tok), emb.T, teach)  76.5 us
    pallas_call x1, Pallas kernels, device_fn(): dh, det, dw = finish(tok, dim, emb.shape[0], dim // nd)(dh, det, dw)  3.69 us

profile of v3, /device:TPU:1, one launch (start us, length us, event | category | flops | bytes accessed | tf_op | source)
XLA Modules:
  0.0 82.5 jit_solution(6060141899989145012)
XLA Ops:
  0.6 76.5 %head.1 = (f32[1,1]{1,0:T(1,128)}, bf16[576,1024]{1,0:T(8,128)(2,1)}, f32[72,3072]{1,0:T(8,128)}, f32[1,576]{1,0:T(1,128)}) custom-call(bf16[576,1024]{1,0:T(8,128)(2,1)} %bitcast.7, bf16[576]{0:T(1024)(128)(2,1)} %w_ref.1, s32[1,1024]{1,0:T(1,128)} %bitcast.8, bf16[576,3072]{1,0:T(8,128)(2,1)} %bitcast.6, bf16[1024,3072]{1,0:T(8,128)(2,1)} %t_hbm.1), custom_call_target="tpu_custom_call" | custom-call | tf_op jit(solution)/shard_map/head/pallas_call | solution.py:546
  77.1 3.7 %finish.1 = (bf16[576,1024]{1,0:T(8,128)(2,1)}, f32[72,3072]{1,0:T(8,128)}, f32[576]{0:T(1024)}) custom-call(bf16[576,1024]{1,0:T(8,128)(2,1)} %get-tuple-element.12.dh, f32[72,3072]{1,0:T(8,128)} %get-tuple-element.13.det, f32[1,576]{1,0:T(1,128)} %get-tuple-element.14.dw), custom_call_target="tpu_custom_call" | custom-call | tf_op jit(solution)/shard_map/finish/pallas_call | solution.py:547
